TPU v7x, 32 devices: a whole 2x2x4 slice. The times are simulated.
32 devices in a mesh: nodes: 2 (over core), gx: 4 (over z), gy: 4 (over y, x).
Axes of the slice: x: 2, y: 2, z: 4, core: 2. Of those that a mesh axis runs over, the one named last changes fastest.
Arguments:
- field_modes: float32 [4, 9, 256, 512], P(None, None, 'gx', 'gy'), may hold values from -4 to 4, as said below
- node_points: float32 [768, 8], replicated, may hold values from -1 to 1
- quad_weight: float32 [768], replicated, may hold values from 0.5 to 2
- group_of: int32 [768], replicated, may hold values from 0 to 2, as said below
Outputs:
- mean_field: float32 [256, 512], P('gx', 'gy')
- variance_field: float32 [256, 512], P('gx', 'gy')
Inputs may be any that keep to these rules, and one draw needn't show every extreme that they name: `group_of`: one of the two groups (which one varies) is given exactly 384 nodes, the other between 48 and 96; all other nodes hold 2. `field_modes`: diffusivity fields (index 3) give a diffusivity between 0.1 and 1.4 at every node point in range; the other fields lie within the range.
All inputs are finite; a program needn't handle non-finite values.
Results may differ from a plain program's by a relative error of at most 0.00021.
Values sent between devices are 32-bit elements; how exact they have to be, the bound alone decides.
No kernel may reach another device: no remote copies, remote signals or barrier semaphores. Data moves between devices by JAX's collectives and lax.ppermute only.
A program may use at most 192 MiB of HBM per device.

v0:
```python
import jax
import jax.numpy as jnp
from jax import lax
from jax.experimental import pallas as pl
from jax.experimental.pallas import tpu as pltpu
from jax.sharding import PartitionSpec as P

STEPS = 4
TIME_STEP = 0.15
LANES = 128
SUBLANES = 8
BLOCK = 4


def split(x):
    high = x.astype(jnp.bfloat16).astype(jnp.float32)
    return high, x - high


def moments_kernel(centre_ref, edge_ref, table_ref, weight_ref, order_ref, out_ref, w_ref, coef_ref, state_ref):
    trips = centre_ref.shape[0] // BLOCK
    cells = order_ref.shape[0]
    slots = table_ref.shape[2]
    kinds = table_ref.shape[0]
    groups = slots // LANES
    out_ref[...] = jnp.zeros_like(out_ref)
    for kind in range(kinds):
        high, low = split(table_ref[kind])
        w_ref[kind] = jnp.concatenate([high, high, low], axis=0).astype(jnp.bfloat16)

    def body(trip, carry):
        def slot(row):
            lag = row // BLOCK
            return ((trip + lag) & 1) * BLOCK + (row - lag * BLOCK)

        lhs = []
        for row in range(BLOCK):
            index = trip * BLOCK + row
            field = jnp.concatenate([centre_ref[index], edge_ref[index]], axis=1)
            high, low = split(field)
            stacked = jnp.concatenate([high, low, high], axis=0).astype(jnp.bfloat16)
            lhs.append(
                lax.dot_general(
                    order_ref[...], stacked, (((1,), (1,)), ((), ())), preferred_element_type=jnp.float32
                )
            )
        lhs = jnp.concatenate(lhs, axis=0).astype(jnp.bfloat16)
        for kind in range(kinds):
            values = jnp.dot(lhs, w_ref[kind], preferred_element_type=jnp.float32)
            for row in range(BLOCK):
                part = values[row * cells : (row + 1) * cells]
                if kind == 0:
                    state_ref[0, slot(row)] = part
                else:
                    coef_ref[kind - 1, slot(row)] = part

        firsts, seconds = [], []
        for step in range(1, STEPS + 1):
            for offset in range(BLOCK):
                row = offset - step
                first = second = None
                for group in range(groups):
                    lanes = pl.ds(group * LANES, LANES)
                    centre = state_ref[step - 1, slot(row), :, lanes]
                    west = state_ref[step - 1, slot(row - 1), :, lanes]
                    east = state_ref[step - 1, slot(row + 1), :, lanes]
                    wrap_north = pltpu.roll(centre[:SUBLANES], SUBLANES - 1, 0)
                    wrap_south = pltpu.roll(centre[cells - SUBLANES :], 1, 0)
                    north = jnp.concatenate([centre[SUBLANES:], wrap_north], axis=0)
                    south = jnp.concatenate([wrap_south, centre[: cells - SUBLANES]], axis=0)
                    c0, ce, cw, cn, cs = (coef_ref[k, slot(row), :, lanes] for k in range(5))
                    new = (c0 * centre + (ce * east + cw * west)) + (cn * north + cs * south)
                    if step < STEPS:
                        state_ref[step, slot(row), :, lanes] = new
                    else:
                        scaled = new * weight_ref[:, lanes]
                        squared = scaled * new
                        first = scaled if first is None else first + scaled
                        second = squared if second is None else second + squared
                if step == STEPS:
                    firsts.append(first)
                    seconds.append(second)

        @pl.when(trip * BLOCK >= 2 * STEPS)
        def _():
            column = lax.broadcasted_iota(jnp.int32, (cells, out_ref.shape[2]), 1)
            base = trip * BLOCK - 2 * STEPS
            for which, sums in enumerate((firsts, seconds)):
                kept = out_ref[which]
                for offset in range(BLOCK):
                    total = jnp.sum(sums[offset], axis=1, keepdims=True)
                    kept = jnp.where(column == base + offset, total, kept)
                out_ref[which] = kept

        return carry

    lax.fori_loop(0, trips, body, 0)


def on_device(field_modes, node_points, quad_weight, group_of):
    kinds, modes, tile_rows, tile_cols = field_modes.shape
    node_count = group_of.shape[0]
    members = lax.axis_size("nodes")
    most = node_count // 2 + node_count // 8
    slots = -(-most // (members * LANES)) * LANES
    member = lax.axis_index("nodes")

    included = group_of < 2
    weight = quad_weight * included.astype(jnp.float32)
    number = jnp.arange(node_count, dtype=jnp.int32)
    before = (number[None, :] < number[:, None]) & included[None, :]
    position = jnp.sum(before.astype(jnp.float32), axis=1).astype(jnp.int32)
    target = jnp.arange(slots, dtype=jnp.int32) * members + member
    select = (included[:, None] & (position[:, None] == target[None, :])).astype(jnp.float32)
    columns = jnp.concatenate([jnp.ones((node_count, 1), jnp.float32), node_points, quad_weight[:, None]], axis=1)
    chosen = lax.dot_general(columns, select, (((0,), (0,)), ((), ())), precision=lax.Precision.HIGHEST)
    slot_coeff, slot_weight = chosen[: modes], chosen[modes:]
    half = 0.5 * TIME_STEP
    mix = (
        ((1.0, 0.0, 0.0, 0.0), 0.0),
        ((0.0, 0.0, 0.0, -4.0 * TIME_STEP), 1.0),
        ((0.0, -half, 0.0, TIME_STEP), 0.0),
        ((0.0, half, 0.0, TIME_STEP), 0.0),
        ((0.0, 0.0, -half, TIME_STEP), 0.0),
        ((0.0, 0.0, half, TIME_STEP), 0.0),
    )
    used = kinds * modes
    padded = -(-(used + 1) // SUBLANES) * SUBLANES
    mixes = jnp.array([m for m, _ in mix], jnp.float32)
    constant = jnp.array([c for _, c in mix], jnp.float32)
    table = (mixes[:, :, None, None] * slot_coeff[None, None]).reshape(len(mix), used, slots)
    table = jnp.concatenate(
        [
            table,
            jnp.broadcast_to(constant[:, None, None], (len(mix), 1, slots)),
            jnp.zeros((len(mix), padded - used - 1, slots), jnp.float32),
        ],
        axis=1,
    )

    def ring(axis):
        size = lax.axis_size(axis)
        up = [(i, (i + 1) % size) for i in range(size)]
        return up, [(j, i) for i, j in up]

    fields = field_modes.reshape(used, tile_rows, tile_cols)
    up, down = ring("gx")
    above = lax.ppermute(fields[:, tile_rows - STEPS :], "gx", up)
    below = lax.ppermute(fields[:, :STEPS], "gx", down)
    tall = jnp.concatenate([above, fields, below], axis=1)
    up, down = ring("gy")
    left = lax.ppermute(jnp.transpose(tall[:, :, tile_cols - STEPS :], (2, 0, 1)), "gy", up)
    right = lax.ppermute(jnp.transpose(tall[:, :, :STEPS], (2, 0, 1)), "gy", down)
    edge = jnp.transpose(jnp.concatenate([left, right], axis=0), (2, 1, 0))
    centre = jnp.transpose(tall, (1, 0, 2))
    fill = ((0, 0), (0, padded - used), (0, 0))
    centre = jnp.pad(centre, fill, constant_values=1.0)
    edge = jnp.pad(edge, fill, constant_values=1.0)

    cells = tile_cols + 2 * STEPS
    per = cells // SUBLANES
    place = jnp.arange(cells, dtype=jnp.int32)
    wanted = (place % SUBLANES) * per + place // SUBLANES - STEPS
    source = jnp.where(
        wanted < 0, tile_cols + STEPS + wanted, jnp.where(wanted < tile_cols, wanted, wanted + STEPS)
    )
    order = (source[:, None] == place[None, :]).astype(jnp.bfloat16)

    sums = pl.pallas_call(
        moments_kernel,
        out_shape=jax.ShapeDtypeStruct((2, cells, tile_rows), jnp.float32),
        scratch_shapes=[
            pltpu.VMEM((len(mix), 3 * padded, slots), jnp.bfloat16),
            pltpu.VMEM((5, 2 * BLOCK, cells, slots), jnp.float32),
            pltpu.VMEM((STEPS, 2 * BLOCK, cells, slots), jnp.float32),
        ],
        compiler_params=pltpu.CompilerParams(vmem_limit_bytes=48 * 1024 * 1024),
        name="moments",
    )(centre, edge, table, slot_weight, order)

    total = sums
    for shift in range(1, members):
        ring_pairs = [(i, (i + shift) % members) for i in range(members)]
        total = total + lax.ppermute(sums, "nodes", ring_pairs)
    weight_total = jnp.sum(weight)
    mean = total[0] / weight_total
    variance = total[1] / weight_total - mean * mean
    fields_out = jnp.stack([mean, variance]).reshape(2, per, SUBLANES, tile_rows)
    fields_out = jnp.transpose(fields_out, (0, 3, 2, 1)).reshape(2, tile_rows, cells)
    fields_out = fields_out[:, :, STEPS : STEPS + tile_cols]
    return fields_out[0], fields_out[1]


def solution(mesh):
    placed = (P(None, None, "gx", "gy"), P(), P(), P())
    return jax.shard_map(
        on_device,
        mesh=mesh,
        in_specs=placed,
        out_specs=(P("gx", "gy"), P("gx", "gy")),
        check_vma=False,
    )
```

profile of v0, /device:TPU:0, one launch (start us, length us, event | category | flops | bytes accessed | tf_op | source)
XLA Modules:
  0.0 61.5 jit_solution(16254288358650374846)
XLA Ops:
  0.7 1.1 %fusion.19 = (f32[36,4,128]{2,1,0:T(4,128)S(1)}, f32[36,4,128]{2,1,0:T(4,128)S(1)}) fusion(f32[36,64,128]{2,1,0:T(8,128)} %bitcast.20), kind=kLoop, calls=%fused_computation.44 | loop fusion | bytes 294912 | tf_op jit(solution)/shard_map/slice | solution.py:149
  1.8 3.1 %collective-permute-start = (f32[36,4,128]{2,0,1:T(8,128)S(1)}, f32[36,4,128]{2,0,1:T(8,128)S(1)}, u32[]{:S(2)}, u32[]{:S(2)}) collective-permute-start(f32[36,4,128]{2,0,1:T(8,128)S(1)} %copy.38), channel_id=1, source_target_pairs={{0,4},{4,8},{8,12},{12,0},{1,5},{5,9},{9,13},{13,1},{2,6},{6,10},{... | collective-permute-start | bytes 221192 | tf_op jit(solution)/shard_map/ppermute | solution.py:148
  4.9 2.1 %collective-permute-start.1 = (f32[36,4,128]{2,0,1:T(8,128)S(1)}, f32[36,4,128]{2,0,1:T(8,128)S(1)}, u32[]{:S(2)}, u32[]{:S(2)}) collective-permute-start(f32[36,4,128]{2,0,1:T(8,128)S(1)} %copy.39), channel_id=1, source_target_pairs={{4,0},{8,4},{12,8},{0,12},{5,1},{9,5},{13,9},{1,13},{6,2},{10,6},{... | collective-permute-start | bytes 221192 | tf_op jit(solution)/shard_map/ppermute | solution.py:149
  7.0 0.7 %broadcast_in_dim.9 = f32[768,1]{0,1:T(1,128)S(1)} reshape(f32[768]{0:T(1024)} %param.8) | data formatting | bytes 6144 | tf_op jit(solution)/shard_map/broadcast_in_dim | solution.py:115
  7.7 1.3 %select_reduce_fusion = (f32[]{:T(128)}, pred[768]{0:T(1024)(128)(4,1)S(1)}) fusion(f32[768]{0:T(1024)} %param.8, s32[768]{0:T(1024)} %param.9), kind=kLoop, calls=%fused_computation.29 | loop fusion | flops 2303 | bytes 6916 | tf_op jit(solution)/shard_map/reduce_sum | solution.py:185
  9.0 0.2 convert_reduce_fusion
  9.2 1.2 %fusion.1 = f32[10,256]{1,0:T(8,128)S(1)} fusion(s32[256]{0:T(256)S(1)} %multiply_add_fusion, s32[768]{0:T(1024)S(1)} %convert_element_type.16, pred[768]{0:T(1024)(128)(4,1)S(1)} %get-tuple-element.9, f32[768,1]{0,1:T(1,128)S(1)} %broadcast_in_dim.9, f32[768,8]{0,1:T(8,128)} %param.7, f32[10]{0:T(128)S(1)} %pad.15.clone), kind=kOutput, calls=%fused_computation.6 | convolution fusion | flops 24001536 | bytes 42792 | tf_op jit(solution)/shard_map/dot_general | solution.py:116
  10.5 0.8 %mul.49 = f32[6,4,9]{2,1,0:T(4,128)S(1)} broadcast(f32[6,4]{1,0:T(8,128)} %constant.62.clone), dimensions={0,1} | broadcast | bytes 960 | tf_op jit(solution)/shard_map/mul | solution.py:131
  11.2 0.1 mul.50
  11.3 0.1 pad.14.clone
  11.4 0.1 broadcast_multiply_fusion
  11.6 0.1 maximum_maximum_fusion.table_ref
  11.7 0.7 %constant_dynamic-update-slice_fusion.1 = f32[36,72,128]{2,0,1:T(8,128)S(1)} fusion(f32[36,72,128]{2,0,1:T(8,128)S(1)} %constant_dynamic-update-slice_fusion.2, f32[36,64,128]{2,1,0:T(8,128)S(1)} %bitcast.21), kind=kLoop, calls=%fused_computation.27 | loop fusion | bytes 2490368
  12.5 1.6 %slice_bitcast_fusion.1 = (f32[4,36,72]{0,1,2:T(8,128)}, f32[4,36,72]{0,1,2:T(8,128)S(1)}) fusion(f32[36,72,128]{2,0,1:T(8,128)S(1)} %constant_dynamic-update-slice_fusion), kind=kLoop, calls=%fused_computation.4 | loop fusion | bytes 165888 | tf_op jit(solution)/shard_map/transpose | solution.py:152
  14.0 1.8 %copy.30 = f32[4,36,72]{2,0,1:T(4,128)S(1)} copy(f32[4,36,72]{0,1,2:T(8,128)} %get-tuple-element.10) | data formatting | bytes 82944 | tf_op jit(solution)/shard_map/transpose | solution.py:152
  15.9 1.7 %collective-permute-start.2 = (f32[4,36,72]{2,0,1:T(4,128)S(1)}, f32[4,36,72]{2,0,1:T(4,128)S(1)}, u32[]{:S(2)}, u32[]{:S(2)}) collective-permute-start(f32[4,36,72]{2,0,1:T(4,128)S(1)} %copy.30), channel_id=1, source_target_pairs={{0,1},{1,2},{2,3},{3,0},{4,5},{5,6},{6,7},{7,4},{8,9},{9,10},{10,1... | collective-permute-start | bytes 124424 | tf_op jit(solution)/shard_map/ppermute | solution.py:152
  17.6 0.5 copy.31
  18.1 1.3 %collective-permute-start.3 = (f32[4,36,72]{2,0,1:T(4,128)S(1)}, f32[4,36,72]{2,0,1:T(4,128)S(1)}, u32[]{:S(2)}, u32[]{:S(2)}) collective-permute-start(f32[4,36,72]{2,0,1:T(4,128)S(1)} %copy.31), channel_id=1, source_target_pairs={{1,0},{2,1},{3,2},{0,3},{5,4},{6,5},{7,6},{4,7},{9,8},{10,9},{11,1... | collective-permute-start | bytes 124424 | tf_op jit(solution)/shard_map/ppermute | solution.py:153
  19.3 0.1 fusion.5.order_ref
  19.4 0.1 pad.8.centre_ref
  19.5 2.1 %collective-permute-done.2 = f32[4,36,72]{2,0,1:T(4,128)S(1)} collective-permute-done((f32[4,36,72]{2,0,1:T(4,128)S(1)}, f32[4,36,72]{2,0,1:T(4,128)S(1)}, u32[]{:S(2)}, u32[]{:S(2)}) %collective-permute-start.2) | collective-permute-done | bytes 41504 | tf_op jit(solution)/shard_map/ppermute | solution.py:152
  21.6 0.9 %collective-permute-done.3 = f32[4,36,72]{2,0,1:T(4,128)S(1)} collective-permute-done((f32[4,36,72]{2,0,1:T(4,128)S(1)}, f32[4,36,72]{2,0,1:T(4,128)S(1)}, u32[]{:S(2)}, u32[]{:S(2)}) %collective-permute-start.3) | collective-permute-done | bytes 41504 | tf_op jit(solution)/shard_map/ppermute | solution.py:153
  22.5 0.5 copy.32
  23.0 0.1 pad.9.edge_ref
  23.1 34.4 %moments.1 = f32[2,136,64]{2,1,0:T(8,128)S(1)} custom-call(f32[72,40,128]{2,1,0:T(8,128)S(1)} %pad.8.centre_ref, f32[72,40,8]{2,1,0:T(8,128)S(1)} %pad.9.edge_ref, f32[6,40,256]{2,1,0:T(8,128)S(1)} %maximum_maximum_fusion.table_ref, f32[1,256]{1,0:T(1,128)S(1)} %slice.48.weight_ref, bf16[136,136]{1,0:T(8,128)(2,1)S(1)} %fusion.5.order_ref), custom_call_target="tpu_custom_call" | custom-call | tf_op jit(solution)/shard_map/moments/pallas_call | solution.py:169
  57.6 1.3 %collective-permute-done.4 = f32[2,136,64]{2,1,0:T(8,128)S(1)} collective-permute-done((f32[2,136,64]{2,1,0:T(8,128)S(1)}, f32[2,136,64]{2,1,0:T(8,128)S(1)}, u32[]{:S(2)}, u32[]{:S(2)}) %collective-permute-start.4) | collective-permute-done | bytes 69664 | tf_op jit(solution)/shard_map/ppermute | solution.py:184
  59.0 0.7 %fusion.13 = (f32[1,17,8,64]{3,2,1,0:T(8,128)S(1)}, f32[1,17,8,64]{3,2,1,0:T(8,128)S(1)}) fusion(f32[]{:T(128)} %get-tuple-element.8, f32[2,136,64]{2,1,0:T(8,128)S(1)} %add.69), kind=kLoop, calls=%fused_computation.25 | loop fusion | flops 34816 | bytes 139268 | tf_op jit(solution)/shard_map/stack | solution.py:188
  59.6 0.1 copy.33
  59.8 0.2 pad_maximum_fusion.1
  60.0 0.1 fusion.20
  60.1 0.7 %copy.35 = f32[64,128]{1,0:T(8,128)} copy(f32[64,128]{0,1:T(8,128)S(1)} %bitcast.24) | data formatting | bytes 65536
  60.8 0.7 %copy.36 = f32[64,128]{1,0:T(8,128)} copy(f32[64,128]{0,1:T(8,128)S(1)} %bitcast.23) | data formatting | bytes 65536
  (23 shorter events, 0.4 us)
Async XLA Ops:
  0.6 10.9 %copy-start.1 = (f32[6]{0:T(128)S(1)}, f32[6]{0:T(128)}, u32[]{:S(2)}) copy-start(f32[6]{0:T(128)} %constant.63.clone) | copy-start | bytes 76
  0.6 11.1 %copy-start = (f32[4,9,64,128]{3,2,1,0:T(8,128)S(1)}, f32[4,9,64,128]{3,2,1,0:T(8,128)}, u32[]{:S(2)}) copy-start(f32[4,9,64,128]{3,2,1,0:T(8,128)} %param.6) | copy-start | bytes 3538948
  1.8 9.9 %collective-permute-start = (f32[36,4,128]{2,0,1:T(8,128)S(1)}, f32[36,4,128]{2,0,1:T(8,128)S(1)}, u32[]{:S(2)}, u32[]{:S(2)}) collective-permute-start(f32[36,4,128]{2,0,1:T(8,128)S(1)} %copy.38), channel_id=1, source_target_pairs={{0,4},{4,8},{8,12},{12,0},{1,5},{5,9},{9,13},{13,1},{2,6},{6,10},{... | collective-permute-start | bytes 221192 | tf_op jit(solution)/shard_map/ppermute | solution.py:148
  4.9 7.5 %collective-permute-start.1 = (f32[36,4,128]{2,0,1:T(8,128)S(1)}, f32[36,4,128]{2,0,1:T(8,128)S(1)}, u32[]{:S(2)}, u32[]{:S(2)}) collective-permute-start(f32[36,4,128]{2,0,1:T(8,128)S(1)} %copy.39), channel_id=1, source_target_pairs={{4,0},{8,4},{12,8},{0,12},{5,1},{9,5},{13,9},{1,13},{6,2},{10,6},{... | collective-permute-start | bytes 221192 | tf_op jit(solution)/shard_map/ppermute | solution.py:149
  15.9 5.7 %collective-permute-start.2 = (f32[4,36,72]{2,0,1:T(4,128)S(1)}, f32[4,36,72]{2,0,1:T(4,128)S(1)}, u32[]{:S(2)}, u32[]{:S(2)}) collective-permute-start(f32[4,36,72]{2,0,1:T(4,128)S(1)} %copy.30), channel_id=1, source_target_pairs={{0,1},{1,2},{2,3},{3,0},{4,5},{5,6},{6,7},{7,4},{8,9},{9,10},{10,1... | collective-permute-start | bytes 124424 | tf_op jit(solution)/shard_map/ppermute | solution.py:152
  18.1 4.4 %collective-permute-start.3 = (f32[4,36,72]{2,0,1:T(4,128)S(1)}, f32[4,36,72]{2,0,1:T(4,128)S(1)}, u32[]{:S(2)}, u32[]{:S(2)}) collective-permute-start(f32[4,36,72]{2,0,1:T(4,128)S(1)} %copy.31), channel_id=1, source_target_pairs={{1,0},{2,1},{3,2},{0,3},{5,4},{6,5},{7,6},{4,7},{9,8},{10,9},{11,1... | collective-permute-start | bytes 124424 | tf_op jit(solution)/shard_map/ppermute | solution.py:153
  57.5 1.4 %collective-permute-start.4 = (f32[2,136,64]{2,1,0:T(8,128)S(1)}, f32[2,136,64]{2,1,0:T(8,128)S(1)}, u32[]{:S(2)}, u32[]{:S(2)}) collective-permute-start(f32[2,136,64]{2,1,0:T(8,128)S(1)} %moments.1), channel_id=1, source_target_pairs={{0,16},{16,0},{1,17},{17,1},{2,18},{18,2},{3,19},{19,3},{4,20},{20... | collective-permute-start | bytes 208904 | tf_op jit(solution)/shard_map/ppermute | solution.py:184
where the time goes:
time: 61.8 us; the launch traced here: 61.5 us
  Pallas kernels  34.4 us (56%)
  local copies, waits for them, and re-layouts  9.81 us (16%)
  starting transfers between devices  8.26 us (13%)
  waiting for transfers between devices  4.26 us (7%)
  other arithmetic  2.65 us (4%)
  matrix products  1.22 us (2%)
  between operations  0.89 us (1%)
    pallas_call x1, Pallas kernels, on_device(): pl.pallas_call(moments_kernel, out_shape=jax.ShapeDtypeStruct((2, cells,...  34.4 us
    transpose x2, local copies, waits for them, and re-layouts, on_device(): jnp.transpose(tall[:, :, tile_cols - STEPS:], (2, 0, 1))  3.42 us
    ppermute x1, starting transfers between devices, on_device(): above = lax.ppermute(fields[:, tile_rows - STEPS:], 'gx', up)  3.1 us
    unnamed x10, local copies, waits for them, and re-layouts  2.12 us
    ppermute x1, starting transfers between devices, on_device(): below = lax.ppermute(fields[:, :STEPS], 'gx', down)  2.1 us
    ppermute x1, waiting for transfers between devices, on_device(): lax.ppermute(jnp.transpose(tall[:, :, tile_cols - STEPS:], (2, 0, 1)), 'g...  2.05 us
    ppermute x1, starting transfers between devices, on_device(): lax.ppermute(jnp.transpose(tall[:, :, tile_cols - STEPS:], (2, 0, 1)), 'g...  1.72 us
    ppermute x1, waiting for transfers between devices, on_device(): total = total + lax.ppermute(sums, 'nodes', ring_pairs)  1.35 us
  transfers between devices with their start and end apart: 5, of which 3 were waited for; matrix products, arithmetic and copies ran while one was open for 10% of the time, Pallas kernels for 0%

commit v1 on v0

--- a/solution.py
+++ b/solution.py
@@ -9,7 +9,9 @@
 TIME_STEP = 0.15
 LANES = 128
 SUBLANES = 8
-BLOCK = 4
+BLOCK = 2
+UNROLL = 4
+RING = BLOCK * UNROLL
 
 
 def split(x):
@@ -17,84 +19,97 @@
     return high, x - high
 
 
-def moments_kernel(centre_ref, edge_ref, table_ref, weight_ref, order_ref, out_ref, w_ref, coef_ref, state_ref):
-    trips = centre_ref.shape[0] // BLOCK
+def moments_kernel(centre_ref, edge_ref, table_ref, weight_ref, order_ref, out_ref, w_ref, lhs_ref, *rings):
+    rows = centre_ref.shape[0]
     cells = order_ref.shape[0]
     slots = table_ref.shape[2]
     kinds = table_ref.shape[0]
     groups = slots // LANES
+    per = cells // SUBLANES
+    states = (rings[0],) + rings[kinds:]
+    coefs = rings[1:kinds]
     out_ref[...] = jnp.zeros_like(out_ref)
     for kind in range(kinds):
         high, low = split(table_ref[kind])
         w_ref[kind] = jnp.concatenate([high, high, low], axis=0).astype(jnp.bfloat16)
-
-    def body(trip, carry):
-        def slot(row):
-            lag = row // BLOCK
-            return ((trip + lag) & 1) * BLOCK + (row - lag * BLOCK)
-
-        lhs = []
+    column = lax.broadcasted_iota(jnp.int32, (SUBLANES, out_ref.shape[2]), 1)
+
+    def left_side(base, half):
+        parts = []
         for row in range(BLOCK):
-            index = trip * BLOCK + row
+            index = jnp.minimum(base + row, rows - 1)
             field = jnp.concatenate([centre_ref[index], edge_ref[index]], axis=1)
             high, low = split(field)
             stacked = jnp.concatenate([high, low, high], axis=0).astype(jnp.bfloat16)
-            lhs.append(
+            parts.append(
                 lax.dot_general(
                     order_ref[...], stacked, (((1,), (1,)), ((), ())), preferred_element_type=jnp.float32
                 )
             )
-        lhs = jnp.concatenate(lhs, axis=0).astype(jnp.bfloat16)
-        for kind in range(kinds):
-            values = jnp.dot(lhs, w_ref[kind], preferred_element_type=jnp.float32)
-            for row in range(BLOCK):
-                part = values[row * cells : (row + 1) * cells]
-                if kind == 0:
-                    state_ref[0, slot(row)] = part
+        lhs_ref[half] = jnp.concatenate(parts, axis=0).astype(jnp.bfloat16)
+
+    def parameter(kind, half):
+        values = jnp.dot(lhs_ref[half], w_ref[kind], preferred_element_type=jnp.float32)
+        for row in range(BLOCK):
+            rings[kind][half * BLOCK + row] = values[row * cells : (row + 1) * cells]
+
+    def tile(ref, row, part, group):
+        return ref[row % RING, part * SUBLANES : (part + 1) * SUBLANES, group * LANES : (group + 1) * LANES]
+
+    def advance(step, row, base):
+        source = states[step - 1]
+        weights = [
+            jnp.broadcast_to(weight_ref[:, g * LANES : (g + 1) * LANES], (SUBLANES, LANES)) for g in range(groups)
+        ]
+        start = [tile(source, row, 0, g) for g in range(groups)]
+        last = [tile(source, row, per - 1, g) for g in range(groups)]
+        south = [pltpu.roll(x, 1, 0) for x in last]
+        wrapped = [pltpu.roll(x, SUBLANES - 1, 0) for x in start]
+        centre = start
+        for part in range(per):
+            first = second = None
+            north = wrapped if part == per - 1 else [tile(source, row, part + 1, g) for g in range(groups)]
+            for g in range(groups):
+                west = tile(source, row - 1, part, g)
+                east = tile(source, row + 1, part, g)
+                c0, ce, cw, cn, cs = (tile(ref, row, part, g) for ref in coefs)
+                fresh = (c0 * centre[g] + (ce * east + cw * west)) + (cn * north[g] + cs * south[g])
+                if step < STEPS:
+                    states[step][
+                        row % RING, part * SUBLANES : (part + 1) * SUBLANES, g * LANES : (g + 1) * LANES
+                    ] = fresh
                 else:
-                    coef_ref[kind - 1, slot(row)] = part
-
-        firsts, seconds = [], []
-        for step in range(1, STEPS + 1):
-            for offset in range(BLOCK):
-                row = offset - step
-                first = second = None
-                for group in range(groups):
-                    lanes = pl.ds(group * LANES, LANES)
-                    centre = state_ref[step - 1, slot(row), :, lanes]
-                    west = state_ref[step - 1, slot(row - 1), :, lanes]
-                    east = state_ref[step - 1, slot(row + 1), :, lanes]
-                    wrap_north = pltpu.roll(centre[:SUBLANES], SUBLANES - 1, 0)
-                    wrap_south = pltpu.roll(centre[cells - SUBLANES :], 1, 0)
-                    north = jnp.concatenate([centre[SUBLANES:], wrap_north], axis=0)
-                    south = jnp.concatenate([wrap_south, centre[: cells - SUBLANES]], axis=0)
-                    c0, ce, cw, cn, cs = (coef_ref[k, slot(row), :, lanes] for k in range(5))
-                    new = (c0 * centre + (ce * east + cw * west)) + (cn * north + cs * south)
-                    if step < STEPS:
-                        state_ref[step, slot(row), :, lanes] = new
-                    else:
-                        scaled = new * weight_ref[:, lanes]
-                        squared = scaled * new
-                        first = scaled if first is None else first + scaled
-                        second = squared if second is None else second + squared
-                if step == STEPS:
-                    firsts.append(first)
-                    seconds.append(second)
-
-        @pl.when(trip * BLOCK >= 2 * STEPS)
-        def _():
-            column = lax.broadcasted_iota(jnp.int32, (cells, out_ref.shape[2]), 1)
-            base = trip * BLOCK - 2 * STEPS
-            for which, sums in enumerate((firsts, seconds)):
-                kept = out_ref[which]
-                for offset in range(BLOCK):
-                    total = jnp.sum(sums[offset], axis=1, keepdims=True)
-                    kept = jnp.where(column == base + offset, total, kept)
-                out_ref[which] = kept
-
+                    scaled = fresh * weights[g]
+                    squared = scaled * fresh
+                    first = scaled if first is None else first + scaled
+                    second = squared if second is None else second + squared
+            south, centre = centre, north
+            if step == STEPS:
+                here = column == base + row - STEPS
+                rows_here = slice(part * SUBLANES, (part + 1) * SUBLANES)
+                for which, sums in enumerate((first, second)):
+                    total = jnp.sum(sums, axis=1, keepdims=True)
+                    out_ref[which, rows_here] = jnp.where(here, total, out_ref[which, rows_here])
+
+    left_side(0, 0)
+    for kind in range(kinds):
+        parameter(kind, 0)
+
+    def body(trip, carry):
+        base = trip * RING
+        for half in range(UNROLL):
+            following = (half + 1) % UNROLL
+            left_side(base + (half + 1) * BLOCK, following)
+            kind = 0
+            units = [(s, half * BLOCK + o - s) for s in range(1, STEPS + 1) for o in range(BLOCK)]
+            for number, (step, row) in enumerate(units):
+                advance(step, row, base)
+                while kind * len(units) < kinds * (number + 1):
+                    parameter(kind, following)
+                    kind += 1
         return carry
 
-    lax.fori_loop(0, trips, body, 0)
+    lax.fori_loop(0, pl.cdiv(rows, RING), body, 0)
 
 
 def on_device(field_modes, node_points, quad_weight, group_of):
@@ -171,9 +186,9 @@
         out_shape=jax.ShapeDtypeStruct((2, cells, tile_rows), jnp.float32),
         scratch_shapes=[
             pltpu.VMEM((len(mix), 3 * padded, slots), jnp.bfloat16),
-            pltpu.VMEM((5, 2 * BLOCK, cells, slots), jnp.float32),
-            pltpu.VMEM((STEPS, 2 * BLOCK, cells, slots), jnp.float32),
-        ],
+            pltpu.VMEM((UNROLL, BLOCK * cells, 3 * padded), jnp.bfloat16),
+        ]
+        + [pltpu.VMEM((RING, cells, slots), jnp.float32)] * (len(mix) + STEPS - 1),
         compiler_params=pltpu.CompilerParams(vmem_limit_bytes=48 * 1024 * 1024),
         name="moments",
     )(centre, edge, table, slot_weight, order)

time: 61.8 us -> 52.8 us (0.85)
  Pallas kernels: 34.4 us -> 25.3 us
    pallas_call x1, Pallas kernels: 34.4 us -> 25.3 us  [on_device(): pl.pallas_call(moments_kernel, out_shape=jax.ShapeDtypeStruct((2, cells,...]
  transfers between devices with their start and end apart: 5 -> 5, of which waited for: 3 -> 3; matrix products, arithmetic and copies ran while one was open for 10% -> 11% of each run, Pallas kernels for 0% -> 0%
where the time goes in v1:
time: 52.8 us; the launch traced here: 52.4 us
  Pallas kernels  25.3 us (48%)
  local copies, waits for them, and re-layouts  9.81 us (19%)
  starting transfers between devices  8.26 us (16%)
  waiting for transfers between devices  4.26 us (8%)
  other arithmetic  2.65 us (5%)
  matrix products  1.22 us (2%)
  between operations  0.89 us (2%)
    pallas_call x1, Pallas kernels, on_device(): pl.pallas_call(moments_kernel, out_shape=jax.ShapeDtypeStruct((2, cells,...  25.3 us
    transpose x2, local copies, waits for them, and re-layouts, on_device(): jnp.transpose(tall[:, :, tile_cols - STEPS:], (2, 0, 1))  3.42 us
    ppermute x1, starting transfers between devices, on_device(): above = lax.ppermute(fields[:, tile_rows - STEPS:], 'gx', up)  3.1 us
    unnamed x10, local copies, waits for them, and re-layouts  2.12 us
    ppermute x1, starting transfers between devices, on_device(): below = lax.ppermute(fields[:, :STEPS], 'gx', down)  2.1 us
    ppermute x1, waiting for transfers between devices, on_device(): lax.ppermute(jnp.transpose(tall[:, :, tile_cols - STEPS:], (2, 0, 1)), 'g...  2.05 us
    ppermute x1, starting transfers between devices, on_device(): lax.ppermute(jnp.transpose(tall[:, :, tile_cols - STEPS:], (2, 0, 1)), 'g...  1.72 us
    ppermute x1, waiting for transfers between devices, on_device(): total = total + lax.ppermute(sums, 'nodes', ring_pairs)  1.35 us
  transfers between devices with their start and end apart: 5, of which 3 were waited for; matrix products, arithmetic and copies ran while one was open for 11% of the time, Pallas kernels for 0%

profile of v1, /device:TPU:0, one launch (start us, length us, event | category | flops | bytes accessed | tf_op | source)
XLA Modules:
  0.0 52.4 jit_solution(1878590665619092501)
XLA Ops:
  0.7 1.1 %fusion.19 = (f32[36,4,128]{2,1,0:T(4,128)S(1)}, f32[36,4,128]{2,1,0:T(4,128)S(1)}) fusion(f32[36,64,128]{2,1,0:T(8,128)} %bitcast.20), kind=kLoop, calls=%fused_computation.44 | loop fusion | bytes 294912 | tf_op jit(solution)/shard_map/slice | solution.py:164
  1.8 3.1 %collective-permute-start = (f32[36,4,128]{2,0,1:T(8,128)S(1)}, f32[36,4,128]{2,0,1:T(8,128)S(1)}, u32[]{:S(2)}, u32[]{:S(2)}) collective-permute-start(f32[36,4,128]{2,0,1:T(8,128)S(1)} %copy.38), channel_id=1, source_target_pairs={{0,4},{4,8},{8,12},{12,0},{1,5},{5,9},{9,13},{13,1},{2,6},{6,10},{... | collective-permute-start | bytes 221192 | tf_op jit(solution)/shard_map/ppermute | solution.py:163
  4.9 2.1 %collective-permute-start.1 = (f32[36,4,128]{2,0,1:T(8,128)S(1)}, f32[36,4,128]{2,0,1:T(8,128)S(1)}, u32[]{:S(2)}, u32[]{:S(2)}) collective-permute-start(f32[36,4,128]{2,0,1:T(8,128)S(1)} %copy.39), channel_id=1, source_target_pairs={{4,0},{8,4},{12,8},{0,12},{5,1},{9,5},{13,9},{1,13},{6,2},{10,6},{... | collective-permute-start | bytes 221192 | tf_op jit(solution)/shard_map/ppermute | solution.py:164
  7.0 0.7 %broadcast_in_dim.9 = f32[768,1]{0,1:T(1,128)S(1)} reshape(f32[768]{0:T(1024)} %param.8) | data formatting | bytes 6144 | tf_op jit(solution)/shard_map/broadcast_in_dim | solution.py:130
  7.7 1.3 %select_reduce_fusion = (f32[]{:T(128)}, pred[768]{0:T(1024)(128)(4,1)S(1)}) fusion(f32[768]{0:T(1024)} %param.8, s32[768]{0:T(1024)} %param.9), kind=kLoop, calls=%fused_computation.29 | loop fusion | flops 2303 | bytes 6916 | tf_op jit(solution)/shard_map/reduce_sum | solution.py:200
  9.0 0.2 convert_reduce_fusion
  9.2 1.2 %fusion.1 = f32[10,256]{1,0:T(8,128)S(1)} fusion(s32[256]{0:T(256)S(1)} %multiply_add_fusion, s32[768]{0:T(1024)S(1)} %convert_element_type.16, pred[768]{0:T(1024)(128)(4,1)S(1)} %get-tuple-element.9, f32[768,1]{0,1:T(1,128)S(1)} %broadcast_in_dim.9, f32[768,8]{0,1:T(8,128)} %param.7, f32[10]{0:T(128)S(1)} %pad.15.clone), kind=kOutput, calls=%fused_computation.6 | convolution fusion | flops 24001536 | bytes 42792 | tf_op jit(solution)/shard_map/dot_general | solution.py:131
  10.5 0.8 %mul.49 = f32[6,4,9]{2,1,0:T(4,128)S(1)} broadcast(f32[6,4]{1,0:T(8,128)} %constant.62.clone), dimensions={0,1} | broadcast | bytes 960 | tf_op jit(solution)/shard_map/mul | solution.py:146
  11.2 0.1 mul.50
  11.3 0.1 pad.14.clone
  11.4 0.1 broadcast_multiply_fusion
  11.6 0.1 maximum_maximum_fusion.table_ref
  11.7 0.7 %constant_dynamic-update-slice_fusion.1 = f32[36,72,128]{2,0,1:T(8,128)S(1)} fusion(f32[36,72,128]{2,0,1:T(8,128)S(1)} %constant_dynamic-update-slice_fusion.2, f32[36,64,128]{2,1,0:T(8,128)S(1)} %bitcast.21), kind=kLoop, calls=%fused_computation.27 | loop fusion | bytes 2490368
  12.5 1.6 %slice_bitcast_fusion.1 = (f32[4,36,72]{0,1,2:T(8,128)}, f32[4,36,72]{0,1,2:T(8,128)S(1)}) fusion(f32[36,72,128]{2,0,1:T(8,128)S(1)} %constant_dynamic-update-slice_fusion), kind=kLoop, calls=%fused_computation.4 | loop fusion | bytes 165888 | tf_op jit(solution)/shard_map/transpose | solution.py:167
  14.0 1.8 %copy.30 = f32[4,36,72]{2,0,1:T(4,128)S(1)} copy(f32[4,36,72]{0,1,2:T(8,128)} %get-tuple-element.10) | data formatting | bytes 82944 | tf_op jit(solution)/shard_map/transpose | solution.py:167
  15.9 1.7 %collective-permute-start.2 = (f32[4,36,72]{2,0,1:T(4,128)S(1)}, f32[4,36,72]{2,0,1:T(4,128)S(1)}, u32[]{:S(2)}, u32[]{:S(2)}) collective-permute-start(f32[4,36,72]{2,0,1:T(4,128)S(1)} %copy.30), channel_id=1, source_target_pairs={{0,1},{1,2},{2,3},{3,0},{4,5},{5,6},{6,7},{7,4},{8,9},{9,10},{10,1... | collective-permute-start | bytes 124424 | tf_op jit(solution)/shard_map/ppermute | solution.py:167
  17.6 0.5 copy.31
  18.1 1.3 %collective-permute-start.3 = (f32[4,36,72]{2,0,1:T(4,128)S(1)}, f32[4,36,72]{2,0,1:T(4,128)S(1)}, u32[]{:S(2)}, u32[]{:S(2)}) collective-permute-start(f32[4,36,72]{2,0,1:T(4,128)S(1)} %copy.31), channel_id=1, source_target_pairs={{1,0},{2,1},{3,2},{0,3},{5,4},{6,5},{7,6},{4,7},{9,8},{10,9},{11,1... | collective-permute-start | bytes 124424 | tf_op jit(solution)/shard_map/ppermute | solution.py:168
  19.3 0.1 fusion.5.order_ref
  19.4 0.1 pad.8.centre_ref
  19.5 2.1 %collective-permute-done.2 = f32[4,36,72]{2,0,1:T(4,128)S(1)} collective-permute-done((f32[4,36,72]{2,0,1:T(4,128)S(1)}, f32[4,36,72]{2,0,1:T(4,128)S(1)}, u32[]{:S(2)}, u32[]{:S(2)}) %collective-permute-start.2) | collective-permute-done | bytes 41504 | tf_op jit(solution)/shard_map/ppermute | solution.py:167
  21.6 0.9 %collective-permute-done.3 = f32[4,36,72]{2,0,1:T(4,128)S(1)} collective-permute-done((f32[4,36,72]{2,0,1:T(4,128)S(1)}, f32[4,36,72]{2,0,1:T(4,128)S(1)}, u32[]{:S(2)}, u32[]{:S(2)}) %collective-permute-start.3) | collective-permute-done | bytes 41504 | tf_op jit(solution)/shard_map/ppermute | solution.py:168
  22.5 0.5 copy.32
  23.0 0.1 pad.9.edge_ref
  23.1 25.3 %moments.1 = f32[2,136,64]{2,1,0:T(8,128)S(1)} custom-call(f32[72,40,128]{2,1,0:T(8,128)S(1)} %pad.8.centre_ref, f32[72,40,8]{2,1,0:T(8,128)S(1)} %pad.9.edge_ref, f32[6,40,256]{2,1,0:T(8,128)S(1)} %maximum_maximum_fusion.table_ref, f32[1,256]{1,0:T(1,128)S(1)} %slice.48.weight_ref, bf16[136,136]{1,0:T(8,128)(2,1)S(1)} %fusion.5.order_ref), custom_call_target="tpu_custom_call" | custom-call | tf_op jit(solution)/shard_map/moments/pallas_call | solution.py:184
  48.5 1.3 %collective-permute-done.4 = f32[2,136,64]{2,1,0:T(8,128)S(1)} collective-permute-done((f32[2,136,64]{2,1,0:T(8,128)S(1)}, f32[2,136,64]{2,1,0:T(8,128)S(1)}, u32[]{:S(2)}, u32[]{:S(2)}) %collective-permute-start.4) | collective-permute-done | bytes 69664 | tf_op jit(solution)/shard_map/ppermute | solution.py:199
  49.9 0.7 %fusion.13 = (f32[1,17,8,64]{3,2,1,0:T(8,128)S(1)}, f32[1,17,8,64]{3,2,1,0:T(8,128)S(1)}) fusion(f32[]{:T(128)} %get-tuple-element.8, f32[2,136,64]{2,1,0:T(8,128)S(1)} %add.69), kind=kLoop, calls=%fused_computation.25 | loop fusion | flops 34816 | bytes 139268 | tf_op jit(solution)/shard_map/stack | solution.py:203
  50.6 0.1 copy.33
  50.8 0.2 pad_maximum_fusion.1
  50.9 0.1 fusion.20
  51.0 0.7 %copy.35 = f32[64,128]{1,0:T(8,128)} copy(f32[64,128]{0,1:T(8,128)S(1)} %bitcast.24) | data formatting | bytes 65536
  51.7 0.7 %copy.36 = f32[64,128]{1,0:T(8,128)} copy(f32[64,128]{0,1:T(8,128)S(1)} %bitcast.23) | data formatting | bytes 65536
  (23 shorter events, 0.4 us)
Async XLA Ops:
  0.6 10.9 %copy-start.1 = (f32[6]{0:T(128)S(1)}, f32[6]{0:T(128)}, u32[]{:S(2)}) copy-start(f32[6]{0:T(128)} %constant.63.clone) | copy-start | bytes 76
  0.6 11.1 %copy-start = (f32[4,9,64,128]{3,2,1,0:T(8,128)S(1)}, f32[4,9,64,128]{3,2,1,0:T(8,128)}, u32[]{:S(2)}) copy-start(f32[4,9,64,128]{3,2,1,0:T(8,128)} %param.6) | copy-start | bytes 3538948
  1.8 9.9 %collective-permute-start = (f32[36,4,128]{2,0,1:T(8,128)S(1)}, f32[36,4,128]{2,0,1:T(8,128)S(1)}, u32[]{:S(2)}, u32[]{:S(2)}) collective-permute-start(f32[36,4,128]{2,0,1:T(8,128)S(1)} %copy.38), channel_id=1, source_target_pairs={{0,4},{4,8},{8,12},{12,0},{1,5},{5,9},{9,13},{13,1},{2,6},{6,10},{... | collective-permute-start | bytes 221192 | tf_op jit(solution)/shard_map/ppermute | solution.py:163
  4.9 7.5 %collective-permute-start.1 = (f32[36,4,128]{2,0,1:T(8,128)S(1)}, f32[36,4,128]{2,0,1:T(8,128)S(1)}, u32[]{:S(2)}, u32[]{:S(2)}) collective-permute-start(f32[36,4,128]{2,0,1:T(8,128)S(1)} %copy.39), channel_id=1, source_target_pairs={{4,0},{8,4},{12,8},{0,12},{5,1},{9,5},{13,9},{1,13},{6,2},{10,6},{... | collective-permute-start | bytes 221192 | tf_op jit(solution)/shard_map/ppermute | solution.py:164
  15.9 5.7 %collective-permute-start.2 = (f32[4,36,72]{2,0,1:T(4,128)S(1)}, f32[4,36,72]{2,0,1:T(4,128)S(1)}, u32[]{:S(2)}, u32[]{:S(2)}) collective-permute-start(f32[4,36,72]{2,0,1:T(4,128)S(1)} %copy.30), channel_id=1, source_target_pairs={{0,1},{1,2},{2,3},{3,0},{4,5},{5,6},{6,7},{7,4},{8,9},{9,10},{10,1... | collective-permute-start | bytes 124424 | tf_op jit(solution)/shard_map/ppermute | solution.py:167
  18.1 4.4 %collective-permute-start.3 = (f32[4,36,72]{2,0,1:T(4,128)S(1)}, f32[4,36,72]{2,0,1:T(4,128)S(1)}, u32[]{:S(2)}, u32[]{:S(2)}) collective-permute-start(f32[4,36,72]{2,0,1:T(4,128)S(1)} %copy.31), channel_id=1, source_target_pairs={{1,0},{2,1},{3,2},{0,3},{5,4},{6,5},{7,6},{4,7},{9,8},{10,9},{11,1... | collective-permute-start | bytes 124424 | tf_op jit(solution)/shard_map/ppermute | solution.py:168
  48.5 1.4 %collective-permute-start.4 = (f32[2,136,64]{2,1,0:T(8,128)S(1)}, f32[2,136,64]{2,1,0:T(8,128)S(1)}, u32[]{:S(2)}, u32[]{:S(2)}) collective-permute-start(f32[2,136,64]{2,1,0:T(8,128)S(1)} %moments.1), channel_id=1, source_target_pairs={{0,16},{16,0},{1,17},{17,1},{2,18},{18,2},{3,19},{19,3},{4,20},{20... | collective-permute-start | bytes 208904 | tf_op jit(solution)/shard_map/ppermute | solution.py:199

commit v2 on v1

--- a/solution.py
+++ b/solution.py
@@ -56,40 +56,42 @@
     def tile(ref, row, part, group):
         return ref[row % RING, part * SUBLANES : (part + 1) * SUBLANES, group * LANES : (group + 1) * LANES]
 
-    def advance(step, row, base):
+    def advance(step, top, base):
         source = states[step - 1]
         weights = [
             jnp.broadcast_to(weight_ref[:, g * LANES : (g + 1) * LANES], (SUBLANES, LANES)) for g in range(groups)
         ]
-        start = [tile(source, row, 0, g) for g in range(groups)]
-        last = [tile(source, row, per - 1, g) for g in range(groups)]
-        south = [pltpu.roll(x, 1, 0) for x in last]
-        wrapped = [pltpu.roll(x, SUBLANES - 1, 0) for x in start]
+        block = [(o, g) for g in range(groups) for o in range(BLOCK)]
+        start = {(o, g): tile(source, top + o, 0, g) for o, g in block}
+        wrapped = {k: pltpu.roll(x, SUBLANES - 1, 0) for k, x in start.items()}
+        south = {(o, g): pltpu.roll(tile(source, top + o, per - 1, g), 1, 0) for o, g in block}
         centre = start
         for part in range(per):
-            first = second = None
-            north = wrapped if part == per - 1 else [tile(source, row, part + 1, g) for g in range(groups)]
-            for g in range(groups):
-                west = tile(source, row - 1, part, g)
-                east = tile(source, row + 1, part, g)
+            here = slice(part * SUBLANES, (part + 1) * SUBLANES)
+            north = wrapped
+            if part < per - 1:
+                north = {(o, g): tile(source, top + o, part + 1, g) for o, g in block}
+            sums = {}
+            for o, g in block:
+                row = top + o
+                west = centre[o - 1, g] if o else tile(source, row - 1, part, g)
+                east = centre[o + 1, g] if o < BLOCK - 1 else tile(source, row + 1, part, g)
                 c0, ce, cw, cn, cs = (tile(ref, row, part, g) for ref in coefs)
-                fresh = (c0 * centre[g] + (ce * east + cw * west)) + (cn * north[g] + cs * south[g])
+                fresh = (c0 * centre[o, g] + (ce * east + cw * west)) + (cn * north[o, g] + cs * south[o, g])
                 if step < STEPS:
-                    states[step][
-                        row % RING, part * SUBLANES : (part + 1) * SUBLANES, g * LANES : (g + 1) * LANES
-                    ] = fresh
+                    states[step][row % RING, here, g * LANES : (g + 1) * LANES] = fresh
                 else:
                     scaled = fresh * weights[g]
-                    squared = scaled * fresh
-                    first = scaled if first is None else first + scaled
-                    second = squared if second is None else second + squared
+                    both = (scaled, scaled * fresh)
+                    sums[o] = tuple(x + y for x, y in zip(sums[o], both)) if o in sums else both
             south, centre = centre, north
             if step == STEPS:
-                here = column == base + row - STEPS
-                rows_here = slice(part * SUBLANES, (part + 1) * SUBLANES)
-                for which, sums in enumerate((first, second)):
-                    total = jnp.sum(sums, axis=1, keepdims=True)
-                    out_ref[which, rows_here] = jnp.where(here, total, out_ref[which, rows_here])
+                for which in range(2):
+                    kept = out_ref[which, here]
+                    for o in range(BLOCK):
+                        total = jnp.sum(sums[o][which], axis=1, keepdims=True)
+                        kept = jnp.where(column == base + top + o - STEPS, total, kept)
+                    out_ref[which, here] = kept
 
     left_side(0, 0)
     for kind in range(kinds):
@@ -101,7 +103,7 @@
             following = (half + 1) % UNROLL
             left_side(base + (half + 1) * BLOCK, following)
             kind = 0
-            units = [(s, half * BLOCK + o - s) for s in range(1, STEPS + 1) for o in range(BLOCK)]
+            units = [(s, half * BLOCK - s) for s in range(1, STEPS + 1)]
             for number, (step, row) in enumerate(units):
                 advance(step, row, base)
                 while kind * len(units) < kinds * (number + 1):
@@ -164,8 +166,14 @@
     below = lax.ppermute(fields[:, :STEPS], "gx", down)
     tall = jnp.concatenate([above, fields, below], axis=1)
     up, down = ring("gy")
-    left = lax.ppermute(jnp.transpose(tall[:, :, tile_cols - STEPS :], (2, 0, 1)), "gy", up)
-    right = lax.ppermute(jnp.transpose(tall[:, :, :STEPS], (2, 0, 1)), "gy", down)
+
+
+    def columns_of(start):
+        parts = [jnp.transpose(x[:, :, start : start + STEPS], (2, 0, 1)) for x in (above, fields, below)]
+        return jnp.concatenate(parts, axis=2)
+
+    left = lax.ppermute(columns_of(tile_cols - STEPS), "gy", up)
+    right = lax.ppermute(columns_of(0), "gy", down)
     edge = jnp.transpose(jnp.concatenate([left, right], axis=0), (2, 1, 0))
     centre = jnp.transpose(tall, (1, 0, 2))
     fill = ((0, 0), (0, padded - used), (0, 0))

time: 52.8 us -> 50.9 us (0.964)
  matrix products: 1.22 us -> 0.48 us
  Pallas kernels: 25.3 us -> 24.6 us
    reshape x0 -> x1, local copies, waits for them, and re-layouts: none -> 2.06 us  [on_device(): fields = field_modes.reshape(used, tile_rows, tile_cols)]
    transpose x3 -> x9, local copies, waits for them, and re-layouts: 3.89 us -> 5.07 us  [columns_of(): jnp.transpose(x[:, :, start:start + STEPS], (2, 0, 1))]
    slice x1, local copies, waits for them, and re-layouts: 1.11 us -> 0.01 us  [on_device(): above = lax.ppermute(fields[:, tile_rows - STEPS:], 'gx', up)]
    pallas_call x1, Pallas kernels: 25.3 us -> 24.6 us  [on_device(): pl.pallas_call(moments_kernel, out_shape=jax.ShapeDtypeStruct((2, cells,...]
    dot_general x1, matrix products: 1.22 us -> 0.48 us  [on_device(): lax.dot_general(columns, select, (((0,), (0,)), ((), ())), precision=lax....]
    reduce_sum x1, other arithmetic: 1.31 us -> 0.6 us  [on_device(): weight_total = jnp.sum(weight)]
    unnamed x10 -> x14, local copies, waits for them, and re-layouts: 2.12 us -> 1.42 us
    mul x4, local copies, waits for them, and re-layouts: 0.87 us -> 0.18 us  [on_device(): mixes[:, :, None, None] * slot_coeff[None, None]]
  transfers between devices with their start and end apart: 5 -> 5, of which waited for: 3 -> 3; matrix products, arithmetic and copies ran while one was open for 11% -> 14% of each run, Pallas kernels for 0% -> 0%
where the time goes in v2:
time: 50.9 us; the launch traced here: 50.7 us
  Pallas kernels  24.6 us (48%)
  local copies, waits for them, and re-layouts  9.87 us (19%)
  starting transfers between devices  8.33 us (16%)
  waiting for transfers between devices  4.24 us (8%)
  other arithmetic  2.33 us (5%)
  between operations  0.91 us (2%)
    pallas_call x1, Pallas kernels, on_device(): pl.pallas_call(moments_kernel, out_shape=jax.ShapeDtypeStruct((2, cells,...  24.6 us
    transpose x9, local copies, waits for them, and re-layouts, columns_of(): jnp.transpose(x[:, :, start:start + STEPS], (2, 0, 1))  5.07 us
    ppermute x1, starting transfers between devices, on_device(): above = lax.ppermute(fields[:, tile_rows - STEPS:], 'gx', up)  3.1 us
    ppermute x1, starting transfers between devices, on_device(): below = lax.ppermute(fields[:, :STEPS], 'gx', down)  2.13 us
    reshape x1, local copies, waits for them, and re-layouts, on_device(): fields = field_modes.reshape(used, tile_rows, tile_cols)  2.06 us
    ppermute x1, starting transfers between devices, on_device(): left = lax.ppermute(columns_of(tile_cols - STEPS), 'gy', up)  1.71 us
    ppermute x1, waiting for transfers between devices, on_device(): right = lax.ppermute(columns_of(0), 'gy', down)  1.57 us
    unnamed x14, local copies, waits for them, and re-layouts  1.42 us
  transfers between devices with their start and end apart: 5, of which 3 were waited for; matrix products, arithmetic and copies ran while one was open for 14% of the time, Pallas kernels for 0%

profile of v2, /device:TPU:0, one launch (start us, length us, event | category | flops | bytes accessed | tf_op | source)
XLA Modules:
  0.0 50.7 jit_solution(10348022595680766419)
XLA Ops:
  0.6 2.1 %copy.33 = f32[36,64,128]{2,0,1:T(8,128)S(1)} copy(f32[36,64,128]{2,1,0:T(8,128)} %bitcast.27) | data formatting | bytes 2359296 | tf_op jit(solution)/shard_map/reshape | solution.py:163
  2.7 3.1 %collective-permute-start = (f32[36,4,128]{2,0,1:T(8,128)S(1)}, f32[36,4,128]{2,0,1:T(8,128)S(1)}, u32[]{:S(2)}, u32[]{:S(2)}) collective-permute-start(f32[36,4,128]{2,0,1:T(8,128)S(1)} %get-tuple-element.10), channel_id=1, source_target_pairs={{0,4},{4,8},{8,12},{12,0},{1,5},{5,9},{9,13},{13,1},{2,6},{6,10},{... | collective-permute-start | bytes 221192 | tf_op jit(solution)/shard_map/ppermute | solution.py:165
  5.8 2.1 %collective-permute-start.1 = (f32[36,4,128]{2,0,1:T(8,128)S(1)}, f32[36,4,128]{2,0,1:T(8,128)S(1)}, u32[]{:S(2)}, u32[]{:S(2)}) collective-permute-start(f32[36,4,128]{2,0,1:T(8,128)S(1)} %get-tuple-element.11), channel_id=1, source_target_pairs={{4,0},{8,4},{12,8},{0,12},{5,1},{9,5},{13,9},{1,13},{6,2},{10,6},{... | collective-permute-start | bytes 221192 | tf_op jit(solution)/shard_map/ppermute | solution.py:166
  8.0 1.4 %slice_bitcast_fusion.1 = (f32[4,36,64]{0,2,1:T(8,128)}, f32[4,36,64]{0,2,1:T(8,128)S(1)}) fusion(f32[36,64,128]{2,1,0:T(8,128)S(1)} %bitcast.28), kind=kLoop, calls=%fused_computation.5 | loop fusion | bytes 147456 | tf_op jit(solution)/shard_map/transpose | solution.py:172
  9.5 0.6 %select_reduce_fusion = (f32[]{:T(128)}, pred[768]{0:T(1024)(128)(4,1)S(1)}) fusion(f32[768]{0:T(1024)S(1)} %copy-done.1, s32[768]{0:T(1024)S(1)} %copy-done.2), kind=kLoop, calls=%fused_computation.33 | loop fusion | flops 2303 | bytes 6916 | tf_op jit(solution)/shard_map/reduce_sum | solution.py:208
  10.1 0.2 convert_reduce_fusion
  10.3 0.5 fusion.1
  11.1 0.1 broadcast_multiply_fusion
  11.5 1.7 %copy.37 = f32[4,36,64]{2,0,1:T(4,128)S(1)} copy(f32[4,36,64]{0,2,1:T(8,128)} %get-tuple-element.12) | data formatting | bytes 73728 | tf_op jit(solution)/shard_map/transpose | solution.py:172
  13.1 0.4 copy.40
  13.6 0.1 slice_bitcast_fusion.5
  13.7 0.3 copy.36
  14.1 0.3 copy.38
  14.4 0.1 pad_maximum_fusion.2
  14.6 1.7 %collective-permute-start.2 = (f32[4,36,72]{2,0,1:T(4,128)S(1)}, f32[4,36,72]{2,0,1:T(4,128)S(1)}, u32[]{:S(2)}, u32[]{:S(2)}) collective-permute-start(f32[4,36,72]{2,0,1:T(4,128)S(1)} %pad_maximum_fusion.2), channel_id=1, source_target_pairs={{0,1},{1,2},{2,3},{3,0},{4,5},{5,6},{6,7},{7,4},{8,9},{9,10},{10,1... | collective-permute-start | bytes 124424 | tf_op jit(solution)/shard_map/ppermute | solution.py:175
  16.3 0.3 copy.39
  16.6 0.3 copy.41
  17.0 0.1 pad_maximum_fusion.3
  17.1 1.3 %collective-permute-start.3 = (f32[4,36,72]{2,0,1:T(4,128)S(1)}, f32[4,36,72]{2,0,1:T(4,128)S(1)}, u32[]{:S(2)}, u32[]{:S(2)}) collective-permute-start(f32[4,36,72]{2,0,1:T(4,128)S(1)} %pad_maximum_fusion.3), channel_id=1, source_target_pairs={{1,0},{2,1},{3,2},{0,3},{5,4},{6,5},{7,6},{4,7},{9,8},{10,9},{11,1... | collective-permute-start | bytes 124424 | tf_op jit(solution)/shard_map/ppermute | solution.py:176
  18.4 0.1 maximum_bitcast_fusion
  18.5 0.1 pad.8.centre_ref
  18.6 1.3 %collective-permute-done.2 = f32[4,36,72]{2,0,1:T(4,128)S(1)} collective-permute-done((f32[4,36,72]{2,0,1:T(4,128)S(1)}, f32[4,36,72]{2,0,1:T(4,128)S(1)}, u32[]{:S(2)}, u32[]{:S(2)}) %collective-permute-start.2) | collective-permute-done | bytes 41504 | tf_op jit(solution)/shard_map/ppermute | solution.py:175
  20.0 1.6 %collective-permute-done.3 = f32[4,36,72]{2,0,1:T(4,128)S(1)} collective-permute-done((f32[4,36,72]{2,0,1:T(4,128)S(1)}, f32[4,36,72]{2,0,1:T(4,128)S(1)}, u32[]{:S(2)}, u32[]{:S(2)}) %collective-permute-start.3) | collective-permute-done | bytes 41504 | tf_op jit(solution)/shard_map/ppermute | solution.py:176
  21.6 0.5 %copy.42 = f32[8,36,72]{0,1,2:T(8,128)S(1)} copy(f32[8,36,72]{2,0,1:T(8,128)S(1)} %pad_maximum_fusion) | data formatting | bytes 165888 | tf_op jit(solution)/shard_map/concatenate | solution.py:177
  22.1 0.1 pad.9.edge_ref
  22.2 24.6 %moments.1 = f32[2,136,64]{2,1,0:T(8,128)S(1)} custom-call(f32[72,40,128]{2,1,0:T(8,128)S(1)} %pad.8.centre_ref, f32[72,40,8]{2,1,0:T(8,128)S(1)} %pad.9.edge_ref, f32[6,40,256]{2,1,0:T(8,128)S(1)} %maximum_maximum_fusion.table_ref, f32[1,256]{1,0:T(1,128)S(1)} %slice.68.weight_ref, bf16[136,136]{1,0:T(8,128)(2,1)S(1)} %fusion.5.order_ref), custom_call_target="tpu_custom_call" | custom-call | tf_op jit(solution)/shard_map/moments/pallas_call | solution.py:192
  46.9 1.3 %collective-permute-done.4 = f32[2,136,64]{2,1,0:T(8,128)S(1)} collective-permute-done((f32[2,136,64]{2,1,0:T(8,128)S(1)}, f32[2,136,64]{2,1,0:T(8,128)S(1)}, u32[]{:S(2)}, u32[]{:S(2)}) %collective-permute-start.4) | collective-permute-done | bytes 69664 | tf_op jit(solution)/shard_map/ppermute | solution.py:207
  48.2 0.7 %fusion.13 = (f32[1,17,8,64]{3,2,1,0:T(8,128)S(1)}, f32[1,17,8,64]{3,2,1,0:T(8,128)S(1)}) fusion(f32[]{:T(128)} %get-tuple-element.8, f32[2,136,64]{2,1,0:T(8,128)S(1)} %add.69), kind=kLoop, calls=%fused_computation.32 | loop fusion | flops 34816 | bytes 139268 | tf_op jit(solution)/shard_map/stack | solution.py:211
  49.1 0.2 pad_maximum_fusion.1
  49.2 0.1 fusion.20
  49.3 0.7 %copy.45 = f32[64,128]{1,0:T(8,128)} copy(f32[64,128]{0,1:T(8,128)S(1)} %bitcast.32) | data formatting | bytes 65536
  50.0 0.7 %copy.46 = f32[64,128]{1,0:T(8,128)} copy(f32[64,128]{0,1:T(8,128)S(1)} %bitcast.31) | data formatting | bytes 65536
  (36 shorter events, 0.9 us)
Async XLA Ops:
  0.6 7.4 %copy-start = (f32[4,9,64,128]{3,2,1,0:T(8,128)S(1)}, f32[4,9,64,128]{3,2,1,0:T(8,128)}, u32[]{:S(2)}) copy-start(f32[4,9,64,128]{3,2,1,0:T(8,128)} %param.6) | copy-start | bytes 3538948
  2.7 10.8 %collective-permute-start = (f32[36,4,128]{2,0,1:T(8,128)S(1)}, f32[36,4,128]{2,0,1:T(8,128)S(1)}, u32[]{:S(2)}, u32[]{:S(2)}) collective-permute-start(f32[36,4,128]{2,0,1:T(8,128)S(1)} %get-tuple-element.10), channel_id=1, source_target_pairs={{0,4},{4,8},{8,12},{12,0},{1,5},{5,9},{9,13},{13,1},{2,6},{6,10},{... | collective-permute-start | bytes 221192 | tf_op jit(solution)/shard_map/ppermute | solution.py:165
  5.8 3.6 %copy-start.1 = (f32[768]{0:T(1024)S(1)}, f32[768]{0:T(1024)}, u32[]{:S(2)}) copy-start(f32[768]{0:T(1024)} %param.8) | copy-start | bytes 9220
  5.8 3.6 %copy-start.2 = (s32[768]{0:T(1024)S(1)}, s32[768]{0:T(1024)}, u32[]{:S(2)}) copy-start(s32[768]{0:T(1024)} %param.9) | copy-start | bytes 9220
  5.8 4.5 %copy-start.5 = (f32[768,8]{0,1:T(8,128)S(1)}, f32[768,8]{0,1:T(8,128)}, u32[]{:S(2)}) copy-start(f32[768,8]{0,1:T(8,128)} %param.7) | copy-start | bytes 73732
  5.8 5.0 %copy-start.3 = (f32[6,4]{1,0:T(8,128)S(1)}, f32[6,4]{1,0:T(8,128)}, u32[]{:S(2)}) copy-start(f32[6,4]{1,0:T(8,128)} %constant.62.clone) | copy-start | bytes 292
  5.8 5.3 %copy-start.4 = (f32[6]{0:T(128)S(1)}, f32[6]{0:T(128)}, u32[]{:S(2)}) copy-start(f32[6]{0:T(128)} %constant.63.clone) | copy-start | bytes 76
  5.8 8.2 %collective-permute-start.1 = (f32[36,4,128]{2,0,1:T(8,128)S(1)}, f32[36,4,128]{2,0,1:T(8,128)S(1)}, u32[]{:S(2)}, u32[]{:S(2)}) collective-permute-start(f32[36,4,128]{2,0,1:T(8,128)S(1)} %get-tuple-element.11), channel_id=1, source_target_pairs={{4,0},{8,4},{12,8},{0,12},{5,1},{9,5},{13,9},{1,13},{6,2},{10,6},{... | collective-permute-start | bytes 221192 | tf_op jit(solution)/shard_map/ppermute | solution.py:166
  14.6 5.4 %collective-permute-start.2 = (f32[4,36,72]{2,0,1:T(4,128)S(1)}, f32[4,36,72]{2,0,1:T(4,128)S(1)}, u32[]{:S(2)}, u32[]{:S(2)}) collective-permute-start(f32[4,36,72]{2,0,1:T(4,128)S(1)} %pad_maximum_fusion.2), channel_id=1, source_target_pairs={{0,1},{1,2},{2,3},{3,0},{4,5},{5,6},{6,7},{7,4},{8,9},{9,10},{10,1... | collective-permute-start | bytes 124424 | tf_op jit(solution)/shard_map/ppermute | solution.py:175
  17.1 4.4 %collective-permute-start.3 = (f32[4,36,72]{2,0,1:T(4,128)S(1)}, f32[4,36,72]{2,0,1:T(4,128)S(1)}, u32[]{:S(2)}, u32[]{:S(2)}) collective-permute-start(f32[4,36,72]{2,0,1:T(4,128)S(1)} %pad_maximum_fusion.3), channel_id=1, source_target_pairs={{1,0},{2,1},{3,2},{0,3},{5,4},{6,5},{7,6},{4,7},{9,8},{10,9},{11,1... | collective-permute-start | bytes 124424 | tf_op jit(solution)/shard_map/ppermute | solution.py:176
  46.8 1.4 %collective-permute-start.4 = (f32[2,136,64]{2,1,0:T(8,128)S(1)}, f32[2,136,64]{2,1,0:T(8,128)S(1)}, u32[]{:S(2)}, u32[]{:S(2)}) collective-permute-start(f32[2,136,64]{2,1,0:T(8,128)S(1)} %moments.1), channel_id=1, source_target_pairs={{0,16},{16,0},{1,17},{17,1},{2,18},{18,2},{3,19},{19,3},{4,20},{20... | collective-permute-start | bytes 208904 | tf_op jit(solution)/shard_map/ppermute | solution.py:207
